TPU v7x, 512 devices: a whole 4x4x16 slice. The times are simulated.
512 devices in a mesh: rows: 128 (over x, z_lo, y), cols: 4 (over z_hi, core).
Axes of the slice: x: 4, y: 4, z: 16 (z_hi: 2, z_lo: 8; z = z_hi * 8 + z_lo), core: 2. Of those that a mesh axis runs over, the one named last changes fastest.
Arguments:
- coords: int32 [8, 262144], P(None, ('rows', 'cols')), may hold values from 0 to 4095
- probes: float32 [64, 262144], P(None, ('rows', 'cols')), may hold values from -6 to 6
- lengthscales: float32 [8], replicated, may hold values from 0.15 to 0.25
- amplitude: float32 [1], replicated, may hold values from 0.1 to 0.3
- landmarks: float32 [254, 8, 128], replicated, may hold values from 0 to 1
- coupling: float32 [128, 128], replicated, may hold values from -0.5 to 0.5
Outputs:
- products: float32 [2, 64, 262144], P(None, None, ('rows', 'cols'))
All inputs are finite; a program needn't handle non-finite values.
Results may differ from a plain program's by a relative error of at most 0.0025.
Values may be sent and summed in bfloat16 or wider, within the bound.
No kernel may reach another device: no remote copies, remote signals or barrier semaphores. Data moves between devices by JAX's collectives and lax.ppermute only.
A program may use at most 64 MiB of HBM per device.

v0:
```python
import jax
import jax.numpy as jnp
from jax import lax
from jax.sharding import PartitionSpec as P


def over_pieces(array, axis):
    return lax.all_gather(array, axis).sum(0)


def swapped(array, axis, apart):
    return lax.ppermute(array, axis, [(i, i ^ 1 << apart) for i in range(lax.axis_size(axis))])


def pair_squares(left_points, right_points):
    squared = jnp.zeros((left_points.shape[1], right_points.shape[1]), jnp.float32)
    for component in range(left_points.shape[0]):
        offset = left_points[component][:, None] - right_points[component][None, :]
        squared = squared + offset * offset
    return squared


def on_device(coords, probes, lengthscales, amplitude, landmarks, coupling):
    highest = lax.Precision.HIGHEST
    inverse_scale = 1.0 / lengthscales
    scaled = coords.astype(jnp.float32) * (1.0 / 4096.0) * inverse_scale[:, None]
    strength = amplitude[0]
    signs_half = probes.astype(jnp.bfloat16)
    width = coords.shape[1]
    groups = lax.axis_size("cols")
    rows_index = lax.axis_index("rows")
    levels = lax.axis_size("rows").bit_length() - 1
    leaf_points = lax.all_gather(scaled, "cols", axis=1, tiled=True)
    leaf_signs = lax.all_gather(signs_half, "cols", axis=1, tiled=True)
    accumulated = jnp.zeros((2, probes.shape[0], width), jnp.float32)
    for row_block in range(groups):
        block_points = leaf_points[:, row_block * width : (row_block + 1) * width]
        block_signs = leaf_signs[:, row_block * width : (row_block + 1) * width]
        squared = pair_squares(block_points, scaled)
        kernel = strength * jnp.exp(-0.5 * squared)
        kernel_half = kernel.astype(jnp.bfloat16)
        slope_half = (kernel * squared).astype(jnp.bfloat16)
        accumulated = accumulated + jnp.stack(
            [
                jnp.dot(block_signs, kernel_half, preferred_element_type=jnp.float32),
                jnp.dot(block_signs, slope_half, preferred_element_type=jnp.float32),
            ]
        )
    result = accumulated
    factor_list = []
    dfactor_list = []
    for level in range(levels):
        depth = levels - level
        node = jnp.right_shift(rows_index, level)
        chosen = lax.dynamic_index_in_dim(landmarks, 2**depth - 2 + node, 0, keepdims=False)
        squared = pair_squares(scaled, chosen * inverse_scale[:, None])
        factor = strength * jnp.exp(-0.5 * squared)
        factor_list.append(factor)
        dfactor_list.append(factor * squared)
    factor_stack = jnp.stack(factor_list)
    dfactor_stack = jnp.stack(dfactor_list)
    own_project = jnp.einsum("pn,lnr->lpr", probes, factor_stack, precision=highest)
    own_dproject = jnp.einsum("pn,lnr->lpr", probes, dfactor_stack, precision=highest)
    projections = over_pieces(jnp.stack([own_project, own_dproject], axis=1), "cols")
    siblings = []
    pending = projections
    for level in range(levels):
        partner = swapped(pending[level:], "rows", level)
        siblings.append(partner[0])
        pending = pending.at[level + 1 :].add(partner[1:])
    for level in range(levels):
        sibling_sums = siblings[level]
        is_left = jnp.right_shift(rows_index, level) & 1 == 0
        core = jnp.where(is_left, coupling.T, coupling)
        first = jnp.dot(sibling_sums[0], core, precision=highest)
        second = jnp.dot(sibling_sums[1], core, precision=highest)
        value = jnp.dot(first, factor_stack[level].T, precision=highest)
        slope = jnp.dot(first, dfactor_stack[level].T, precision=highest) + jnp.dot(
            second, factor_stack[level].T, precision=highest
        )
        result = result + jnp.stack([value, slope])
    return result


def solution(mesh):
    in_specs = (P(None, ("rows", "cols")), P(None, ("rows", "cols")), P(), P(), P(), P())
    out_specs = P(None, None, ("rows", "cols"))
    return jax.shard_map(
        on_device, mesh=mesh, in_specs=in_specs, out_specs=out_specs, check_vma=False
    )
```

profile of v0, /device:TPU:8, one launch (start us, length us, event | category | flops | bytes accessed | tf_op | source)
XLA Modules:
  0.0 196.0 jit_solution(11825295575556073980)
XLA Ops:
  14.0 1.2 convolution_bitcast_fusion
  15.2 1.2 convolution_bitcast_fusion.1
  17.2 17.0 %all_gather.12 = f32[8,2048]{1,0:T(8,128)S(1)} all-gather(f32[8,512]{1,0:T(8,128)S(1)} %convert_multiply_fusion), channel_id=1, replica_groups=mesh['rows'=128,'cols'=4] {'cols'}, dimensions={1}, use_global_device_ids=true | all-gather | bytes 81920 | tf_op jit(solution)/shard_map/all_gather | solution.py:33
  34.3 18.0 %all_gather.13 = bf16[64,2048]{1,0:T(8,128)(2,1)S(1)} all-gather(bf16[64,512]{1,0:T(8,128)(2,1)S(1)} %convert_element_type.32), channel_id=1, replica_groups=mesh['rows'=128,'cols'=4] {'cols'}, dimensions={1}, use_global_device_ids=true | all-gather | bytes 327680 | tf_op jit(solution)/shard_map/all_gather | solution.py:34
  52.3 1.1 convolution_bitcast_fusion.3
  53.4 1.2 convolution_bitcast_fusion.2
  54.7 1.1 convolution_bitcast_fusion.5
  55.8 1.2 convolution_bitcast_fusion.4
  58.2 1.2 convolution_bitcast_fusion.6
  59.4 11.6 %all-gather.3.cloned.1.call-done = f32[28,2,64,128]{3,2,0,1:T(8,128)} async-done(((f32[7,2,64,128]{3,2,0,1:T(8,128)}), f32[28,2,64,128]{3,2,0,1:T(8,128)}) %all-gather.3.cloned.1.call-update) | async-done | bytes 1835024 | tf_op jit(solution)/shard_map/all_gather | solution.py:8
  71.1 1.7 reduce_sum.9
  72.7 3.6 %collective-permute-start = (f32[7,2,64,128]{3,2,0,1:T(8,128)S(1)}, f32[7,2,64,128]{3,2,0,1:T(8,128)S(1)}, u32[]{:S(2)}, u32[]{:S(2)}) collective-permute-start(f32[7,2,64,128]{3,2,0,1:T(8,128)S(1)} %reduce_sum.9), channel_id=1, source_target_pairs={{0,4},{4,0},{8,12},{12,8},{16,20},{20,16},{24,28},{28,24},{32,36},... | collective-permute-start | bytes 1376264 | tf_op jit(solution)/shard_map/ppermute | solution.py:12
  77.6 1.2 convolution_bitcast_fusion.8
  78.9 8.4 %collective-permute-done = f32[7,2,64,128]{3,2,0,1:T(8,128)S(1)} collective-permute-done((f32[7,2,64,128]{3,2,0,1:T(8,128)S(1)}, f32[7,2,64,128]{3,2,0,1:T(8,128)S(1)}, u32[]{:S(2)}, u32[]{:S(2)}) %collective-permute-start) | collective-permute-done | bytes 458784 | tf_op jit(solution)/shard_map/ppermute | solution.py:12
  87.3 4.4 %collective-permute-start.1 = (f32[6,2,64,128]{3,2,0,1:T(8,128)S(1)}, f32[6,2,64,128]{3,2,0,1:T(8,128)S(1)}, u32[]{:S(2)}, u32[]{:S(2)}) collective-permute-start(f32[6,2,64,128]{3,2,0,1:T(8,128)S(1)} %slice_add_fusion), channel_id=1, source_target_pairs={{0,8},{4,12},{8,0},{12,4},{16,24},{20,28},{24,16},{28,20},{32,40},... | collective-permute-start | bytes 1179656 | tf_op jit(solution)/shard_map/ppermute | solution.py:12
  95.1 6.0 %collective-permute-done.1 = f32[6,2,64,128]{3,2,0,1:T(8,128)S(1)} collective-permute-done((f32[6,2,64,128]{3,2,0,1:T(8,128)S(1)}, f32[6,2,64,128]{3,2,0,1:T(8,128)S(1)}, u32[]{:S(2)}, u32[]{:S(2)}) %collective-permute-start.1) | collective-permute-done | bytes 393248 | tf_op jit(solution)/shard_map/ppermute | solution.py:12
  101.2 7.4 %collective-permute-start.2 = (f32[5,2,64,128]{3,2,0,1:T(8,128)S(1)}, f32[5,2,64,128]{3,2,0,1:T(8,128)S(1)}, u32[]{:S(2)}, u32[]{:S(2)}) collective-permute-start(f32[5,2,64,128]{3,2,0,1:T(8,128)S(1)} %slice_add_fusion.1), channel_id=1, source_target_pairs={{0,16},{4,20},{8,24},{12,28},{16,0},{20,4},{24,8},{28,12},{32,48},... | collective-permute-start | bytes 983048 | tf_op jit(solution)/shard_map/ppermute | solution.py:12
  112.0 3.0 %collective-permute-done.2 = f32[5,2,64,128]{3,2,0,1:T(8,128)S(1)} collective-permute-done((f32[5,2,64,128]{3,2,0,1:T(8,128)S(1)}, f32[5,2,64,128]{3,2,0,1:T(8,128)S(1)}, u32[]{:S(2)}, u32[]{:S(2)}) %collective-permute-start.2) | collective-permute-done | bytes 327712 | tf_op jit(solution)/shard_map/ppermute | solution.py:12
  115.0 7.8 %collective-permute-start.3 = (f32[4,2,64,128]{3,2,0,1:T(8,128)S(1)}, f32[4,2,64,128]{3,2,0,1:T(8,128)S(1)}, u32[]{:S(2)}, u32[]{:S(2)}) collective-permute-start(f32[4,2,64,128]{3,2,0,1:T(8,128)S(1)} %slice_add_fusion.2), channel_id=1, source_target_pairs={{0,32},{4,36},{8,40},{12,44},{16,48},{20,52},{24,56},{28,60},{32,0... | collective-permute-start | bytes 786440 | tf_op jit(solution)/shard_map/ppermute | solution.py:12
  126.2 6.7 %collective-permute-done.3 = f32[4,2,64,128]{3,2,0,1:T(8,128)S(1)} collective-permute-done((f32[4,2,64,128]{3,2,0,1:T(8,128)S(1)}, f32[4,2,64,128]{3,2,0,1:T(8,128)S(1)}, u32[]{:S(2)}, u32[]{:S(2)}) %collective-permute-start.3) | collective-permute-done | bytes 262176 | tf_op jit(solution)/shard_map/ppermute | solution.py:12
  132.8 21.1 %collective-permute-start.4 = (f32[3,2,64,128]{3,2,0,1:T(8,128)S(1)}, f32[3,2,64,128]{3,2,0,1:T(8,128)S(1)}, u32[]{:S(2)}, u32[]{:S(2)}) collective-permute-start(f32[3,2,64,128]{3,2,0,1:T(8,128)S(1)} %slice_add_fusion.3), channel_id=1, source_target_pairs={{0,64},{4,68},{8,72},{12,76},{16,80},{20,84},{24,88},{28,92},{32,9... | collective-permute-start | bytes 589832 | tf_op jit(solution)/shard_map/ppermute | solution.py:12
  157.3 11.9 %collective-permute-done.4 = f32[3,2,64,128]{3,2,0,1:T(8,128)S(1)} collective-permute-done((f32[3,2,64,128]{3,2,0,1:T(8,128)S(1)}, f32[3,2,64,128]{3,2,0,1:T(8,128)S(1)}, u32[]{:S(2)}, u32[]{:S(2)}) %collective-permute-start.4) | collective-permute-done | bytes 196640 | tf_op jit(solution)/shard_map/ppermute | solution.py:12
  169.2 3.6 %collective-permute-start.5 = (f32[2,2,64,128]{3,2,0,1:T(8,128)S(1)}, f32[2,2,64,128]{3,2,0,1:T(8,128)S(1)}, u32[]{:S(2)}, u32[]{:S(2)}) collective-permute-start(f32[2,2,64,128]{3,2,0,1:T(8,128)S(1)} %slice_add_fusion.4), channel_id=1, source_target_pairs={{0,128},{4,132},{8,136},{12,140},{16,144},{20,148},{24,152},{28,15... | collective-permute-start | bytes 393224 | tf_op jit(solution)/shard_map/ppermute | solution.py:12
  176.6 4.9 %collective-permute-start.6 = (f32[1,2,64,128]{3,2,0,1:T(8,128)S(1)}, f32[1,2,64,128]{3,2,0,1:T(8,128)S(1)}, u32[]{:S(2)}, u32[]{:S(2)}) collective-permute-start(f32[1,2,64,128]{3,2,0,1:T(8,128)S(1)} %slice_add_fusion.5), channel_id=1, source_target_pairs={{0,256},{4,260},{8,264},{12,268},{16,272},{20,276},{24,280},{28,28... | collective-permute-start | bytes 196616 | tf_op jit(solution)/shard_map/ppermute | solution.py:12
  (72 shorter events, 34.8 us)
Async XLA Ops:
  6.5 64.5 %all-gather.3.cloned.1.call-start = ((), (), s32[]{:S(2)}) async-start(), calls=%async_computation | async-start | bytes 2293760 | tf_op jit(solution)/shard_map/all_gather | solution.py:8
  10.2 3.8 %copy-start.1 = (f32[64,512]{1,0:T(8,128)S(1)}, f32[64,512]{1,0:T(8,128)}, u32[]{:S(2)}) copy-start(f32[64,512]{1,0:T(8,128)} %param.19) | copy-start | bytes 393220
  72.7 14.5 %collective-permute-start = (f32[7,2,64,128]{3,2,0,1:T(8,128)S(1)}, f32[7,2,64,128]{3,2,0,1:T(8,128)S(1)}, u32[]{:S(2)}, u32[]{:S(2)}) collective-permute-start(f32[7,2,64,128]{3,2,0,1:T(8,128)S(1)} %reduce_sum.9), channel_id=1, source_target_pairs={{0,4},{4,0},{8,12},{12,8},{16,20},{20,16},{24,28},{28,24},{32,36},... | collective-permute-start | bytes 1376264 | tf_op jit(solution)/shard_map/ppermute | solution.py:12
  76.3 1.2 copy-start
  87.3 13.8 %collective-permute-start.1 = (f32[6,2,64,128]{3,2,0,1:T(8,128)S(1)}, f32[6,2,64,128]{3,2,0,1:T(8,128)S(1)}, u32[]{:S(2)}, u32[]{:S(2)}) collective-permute-start(f32[6,2,64,128]{3,2,0,1:T(8,128)S(1)} %slice_add_fusion), channel_id=1, source_target_pairs={{0,8},{4,12},{8,0},{12,4},{16,24},{20,28},{24,16},{28,20},{32,40},... | collective-permute-start | bytes 1179656 | tf_op jit(solution)/shard_map/ppermute | solution.py:12
  101.2 13.8 %collective-permute-start.2 = (f32[5,2,64,128]{3,2,0,1:T(8,128)S(1)}, f32[5,2,64,128]{3,2,0,1:T(8,128)S(1)}, u32[]{:S(2)}, u32[]{:S(2)}) collective-permute-start(f32[5,2,64,128]{3,2,0,1:T(8,128)S(1)} %slice_add_fusion.1), channel_id=1, source_target_pairs={{0,16},{4,20},{8,24},{12,28},{16,0},{20,4},{24,8},{28,12},{32,48},... | collective-permute-start | bytes 983048 | tf_op jit(solution)/shard_map/ppermute | solution.py:12
  115.0 17.8 %collective-permute-start.3 = (f32[4,2,64,128]{3,2,0,1:T(8,128)S(1)}, f32[4,2,64,128]{3,2,0,1:T(8,128)S(1)}, u32[]{:S(2)}, u32[]{:S(2)}) collective-permute-start(f32[4,2,64,128]{3,2,0,1:T(8,128)S(1)} %slice_add_fusion.2), channel_id=1, source_target_pairs={{0,32},{4,36},{8,40},{12,44},{16,48},{20,52},{24,56},{28,60},{32,0... | collective-permute-start | bytes 786440 | tf_op jit(solution)/shard_map/ppermute | solution.py:12
  132.8 36.4 %collective-permute-start.4 = (f32[3,2,64,128]{3,2,0,1:T(8,128)S(1)}, f32[3,2,64,128]{3,2,0,1:T(8,128)S(1)}, u32[]{:S(2)}, u32[]{:S(2)}) collective-permute-start(f32[3,2,64,128]{3,2,0,1:T(8,128)S(1)} %slice_add_fusion.3), channel_id=1, source_target_pairs={{0,64},{4,68},{8,72},{12,76},{16,80},{20,84},{24,88},{28,92},{32,9... | collective-permute-start | bytes 589832 | tf_op jit(solution)/shard_map/ppermute | solution.py:12
  169.2 7.3 %collective-permute-start.5 = (f32[2,2,64,128]{3,2,0,1:T(8,128)S(1)}, f32[2,2,64,128]{3,2,0,1:T(8,128)S(1)}, u32[]{:S(2)}, u32[]{:S(2)}) collective-permute-start(f32[2,2,64,128]{3,2,0,1:T(8,128)S(1)} %slice_add_fusion.4), channel_id=1, source_target_pairs={{0,128},{4,132},{8,136},{12,140},{16,144},{20,148},{24,152},{28,15... | collective-permute-start | bytes 393224 | tf_op jit(solution)/shard_map/ppermute | solution.py:12
  176.6 8.2 %collective-permute-start.6 = (f32[1,2,64,128]{3,2,0,1:T(8,128)S(1)}, f32[1,2,64,128]{3,2,0,1:T(8,128)S(1)}, u32[]{:S(2)}, u32[]{:S(2)}) collective-permute-start(f32[1,2,64,128]{3,2,0,1:T(8,128)S(1)} %slice_add_fusion.5), channel_id=1, source_target_pairs={{0,256},{4,260},{8,264},{12,268},{16,272},{20,276},{24,280},{28,28... | collective-permute-start | bytes 196616 | tf_op jit(solution)/shard_map/ppermute | solution.py:12
Sparse Core Ops, SparseCore 0:
  17.3 53.6 all-gather.2
where the time goes:
time: 197 us; the launch traced here: 196 us
  starting transfers between devices  52.9 us (27%)
  waiting for transfers between devices  48 us (24%)
  matrix products  35.1 us (18%)
  blocking collectives  35 us (18%)
  between operations  14.5 us (7%)
  other arithmetic  10.3 us (5%)
    ppermute x7, starting transfers between devices, swapped(): lax.ppermute(array, axis, [(i, i ^ 1 << apart) for i in range(lax.axis_si...  52.9 us
    ppermute x7, waiting for transfers between devices, swapped(): lax.ppermute(array, axis, [(i, i ^ 1 << apart) for i in range(lax.axis_si...  36.3 us
    all_gather x1, blocking collectives, on_device(): leaf_signs = lax.all_gather(signs_half, 'cols', axis=1, tiled=True)  18 us
    all_gather x1, blocking collectives, on_device(): leaf_points = lax.all_gather(scaled, 'cols', axis=1, tiled=True)  17 us
    all_gather x1, waiting for transfers between devices, over_pieces(): return lax.all_gather(array, axis).sum(0)  11.6 us
    dot_general x7, matrix products, on_device(): jnp.dot(first, dfactor_stack[level].T, precision=highest)  6.9 us
    dot_general x7, matrix products, on_device(): jnp.dot(second, factor_stack[level].T, precision=highest)  6.89 us
    dot_general x7, matrix products, on_device(): value = jnp.dot(first, factor_stack[level].T, precision=highest)  6.88 us
  transfers between devices with their start and end apart: 8, of which 7 were waited for; matrix products, arithmetic and copies ran while one was open for 15% of the time, Pallas kernels for 0%

commit v1 on v0

--- a/solution.py
+++ b/solution.py
@@ -2,6 +2,7 @@
 import jax.numpy as jnp
 from jax import lax
 from jax.sharding import PartitionSpec as P
+from jax.lax import all_gather
 
 
 def over_pieces(array, axis):
@@ -30,8 +31,11 @@
     groups = lax.axis_size("cols")
     rows_index = lax.axis_index("rows")
     levels = lax.axis_size("rows").bit_length() - 1
-    leaf_points = lax.all_gather(scaled, "cols", axis=1, tiled=True)
-    leaf_signs = lax.all_gather(signs_half, "cols", axis=1, tiled=True)
+    leaf_points, leaf_signs = jnp.split(
+        all_gather(jnp.concatenate([scaled, signs_half], 0), axis_name="cols", axis=1, tiled=True),
+        [scaled.shape[0]],
+        0,
+    )
     accumulated = jnp.zeros((2, probes.shape[0], width), jnp.float32)
     for row_block in range(groups):
         block_points = leaf_points[:, row_block * width : (row_block + 1) * width]

time: 197 us -> 197 us (level)
  the two profiles are of different devices: /device:TPU:8 before, /device:TPU:24 now
where the time goes in v1:
time: 197 us
  waiting for transfers between devices  83.7 us (42%)
  matrix products  35.1 us (18%)
  starting transfers between devices  32.6 us (17%)
  blocking collectives  20.3 us (10%)
  between operations  14.5 us (7%)
  other arithmetic  10.4 us (5%)
    ppermute x7, waiting for transfers between devices, swapped(): lax.ppermute(array, axis, [(i, i ^ 1 << apart) for i in range(lax.axis_si...  45.7 us
    all_gather x1, waiting for transfers between devices, over_pieces(): return lax.all_gather(array, axis).sum(0)  38 us
    ppermute x7, starting transfers between devices, swapped(): lax.ppermute(array, axis, [(i, i ^ 1 << apart) for i in range(lax.axis_si...  32.6 us
    all_gather x1, blocking collectives, on_device(): all_gather(jnp.concatenate([scaled, signs_half], 0), axis_name='cols', ax...  20.3 us
    dot_general x7, matrix products, on_device(): jnp.dot(second, factor_stack[level].T, precision=highest)  6.89 us
    dot_general x7, matrix products, on_device(): jnp.dot(first, dfactor_stack[level].T, precision=highest)  6.89 us
    dot_general x7, matrix products, on_device(): value = jnp.dot(first, factor_stack[level].T, precision=highest)  6.88 us
    dot_general x4, matrix products, on_device(): jnp.dot(block_signs, slope_half, preferred_element_type=jnp.float32)  4.88 us
  transfers between devices with their start and end apart: 8, of which 7 were waited for; matrix products, arithmetic and copies ran while one was open for 15% of the time, Pallas kernels for 0%

profile of v1, /device:TPU:24, one launch (start us, length us, event | category | flops | bytes accessed | tf_op | source)
XLA Modules:
  0.0 196.8 jit_solution(9812842103140789349)
XLA Ops:
  14.0 1.2 convolution_bitcast_fusion
  15.2 1.2 convolution_bitcast_fusion.1
  17.3 20.3 %all_gather.9 = f32[72,2048]{1,0:T(8,128)S(1)} all-gather(f32[72,512]{1,0:T(8,128)S(1)} %pad_maximum_fusion.1), channel_id=1, replica_groups=mesh['rows'=128,'cols'=4] {'cols'}, dimensions={1}, use_global_device_ids=true | all-gather | bytes 737280 | tf_op jit(solution)/shard_map/all_gather | solution.py:35
  38.8 1.2 convolution_bitcast_fusion.2
  40.0 1.1 convolution_bitcast_fusion.5
  41.2 1.2 convolution_bitcast_fusion.4
  42.4 1.1 convolution_bitcast_fusion.7
  43.6 1.2 convolution_bitcast_fusion.6
  44.8 38.0 %all-gather.3.cloned.1.call-done = f32[28,2,64,128]{3,2,0,1:T(8,128)} async-done(((f32[7,2,64,128]{3,2,0,1:T(8,128)}), f32[28,2,64,128]{3,2,0,1:T(8,128)}) %all-gather.3.cloned.1.call-update) | async-done | bytes 1835024 | tf_op jit(solution)/shard_map/all_gather | solution.py:9
  82.8 1.7 reduce_sum.9
  84.4 2.7 %collective-permute-start = (f32[7,2,64,128]{3,2,0,1:T(8,128)S(1)}, f32[7,2,64,128]{3,2,0,1:T(8,128)S(1)}, u32[]{:S(2)}, u32[]{:S(2)}) collective-permute-start(f32[7,2,64,128]{3,2,0,1:T(8,128)S(1)} %reduce_sum.9), channel_id=1, source_target_pairs={{0,4},{4,0},{8,12},{12,8},{16,20},{20,16},{24,28},{28,24},{32,36},... | collective-permute-start | bytes 1376264 | tf_op jit(solution)/shard_map/ppermute | solution.py:13
  87.1 1.1 convolution_bitcast_fusion.9
  88.4 1.2 convolution_bitcast_fusion.8
  89.6 9.3 %collective-permute-done = f32[7,2,64,128]{3,2,0,1:T(8,128)S(1)} collective-permute-done((f32[7,2,64,128]{3,2,0,1:T(8,128)S(1)}, f32[7,2,64,128]{3,2,0,1:T(8,128)S(1)}, u32[]{:S(2)}, u32[]{:S(2)}) %collective-permute-start) | collective-permute-done | bytes 458784 | tf_op jit(solution)/shard_map/ppermute | solution.py:13
  99.0 2.2 %collective-permute-start.1 = (f32[6,2,64,128]{3,2,0,1:T(8,128)S(1)}, f32[6,2,64,128]{3,2,0,1:T(8,128)S(1)}, u32[]{:S(2)}, u32[]{:S(2)}) collective-permute-start(f32[6,2,64,128]{3,2,0,1:T(8,128)S(1)} %slice_add_fusion), channel_id=1, source_target_pairs={{0,8},{4,12},{8,0},{12,4},{16,24},{20,28},{24,16},{28,20},{32,40},... | collective-permute-start | bytes 1179656 | tf_op jit(solution)/shard_map/ppermute | solution.py:13
  104.6 8.3 %collective-permute-done.1 = f32[6,2,64,128]{3,2,0,1:T(8,128)S(1)} collective-permute-done((f32[6,2,64,128]{3,2,0,1:T(8,128)S(1)}, f32[6,2,64,128]{3,2,0,1:T(8,128)S(1)}, u32[]{:S(2)}, u32[]{:S(2)}) %collective-permute-start.1) | collective-permute-done | bytes 393248 | tf_op jit(solution)/shard_map/ppermute | solution.py:13
  112.9 7.5 %collective-permute-start.2 = (f32[5,2,64,128]{3,2,0,1:T(8,128)S(1)}, f32[5,2,64,128]{3,2,0,1:T(8,128)S(1)}, u32[]{:S(2)}, u32[]{:S(2)}) collective-permute-start(f32[5,2,64,128]{3,2,0,1:T(8,128)S(1)} %slice_add_fusion.1), channel_id=1, source_target_pairs={{0,16},{4,20},{8,24},{12,28},{16,0},{20,4},{24,8},{28,12},{32,48},... | collective-permute-start | bytes 983048 | tf_op jit(solution)/shard_map/ppermute | solution.py:13
  123.7 3.0 %collective-permute-done.2 = f32[5,2,64,128]{3,2,0,1:T(8,128)S(1)} collective-permute-done((f32[5,2,64,128]{3,2,0,1:T(8,128)S(1)}, f32[5,2,64,128]{3,2,0,1:T(8,128)S(1)}, u32[]{:S(2)}, u32[]{:S(2)}) %collective-permute-start.2) | collective-permute-done | bytes 327712 | tf_op jit(solution)/shard_map/ppermute | solution.py:13
  126.8 9.7 %collective-permute-start.3 = (f32[4,2,64,128]{3,2,0,1:T(8,128)S(1)}, f32[4,2,64,128]{3,2,0,1:T(8,128)S(1)}, u32[]{:S(2)}, u32[]{:S(2)}) collective-permute-start(f32[4,2,64,128]{3,2,0,1:T(8,128)S(1)} %slice_add_fusion.2), channel_id=1, source_target_pairs={{0,32},{4,36},{8,40},{12,44},{16,48},{20,52},{24,56},{28,60},{32,0... | collective-permute-start | bytes 786440 | tf_op jit(solution)/shard_map/ppermute | solution.py:13
  139.9 6.4 %collective-permute-done.3 = f32[4,2,64,128]{3,2,0,1:T(8,128)S(1)} collective-permute-done((f32[4,2,64,128]{3,2,0,1:T(8,128)S(1)}, f32[4,2,64,128]{3,2,0,1:T(8,128)S(1)}, u32[]{:S(2)}, u32[]{:S(2)}) %collective-permute-start.3) | collective-permute-done | bytes 262176 | tf_op jit(solution)/shard_map/ppermute | solution.py:13
  146.3 1.9 collective-permute-start.4
  151.6 18.4 %collective-permute-done.4 = f32[3,2,64,128]{3,2,0,1:T(8,128)S(1)} collective-permute-done((f32[3,2,64,128]{3,2,0,1:T(8,128)S(1)}, f32[3,2,64,128]{3,2,0,1:T(8,128)S(1)}, u32[]{:S(2)}, u32[]{:S(2)}) %collective-permute-start.4) | collective-permute-done | bytes 196640 | tf_op jit(solution)/shard_map/ppermute | solution.py:13
  169.9 3.7 %collective-permute-start.5 = (f32[2,2,64,128]{3,2,0,1:T(8,128)S(1)}, f32[2,2,64,128]{3,2,0,1:T(8,128)S(1)}, u32[]{:S(2)}, u32[]{:S(2)}) collective-permute-start(f32[2,2,64,128]{3,2,0,1:T(8,128)S(1)} %slice_add_fusion.4), channel_id=1, source_target_pairs={{0,128},{4,132},{8,136},{12,140},{16,144},{20,148},{24,152},{28,15... | collective-permute-start | bytes 393224 | tf_op jit(solution)/shard_map/ppermute | solution.py:13
  177.3 4.9 %collective-permute-start.6 = (f32[1,2,64,128]{3,2,0,1:T(8,128)S(1)}, f32[1,2,64,128]{3,2,0,1:T(8,128)S(1)}, u32[]{:S(2)}, u32[]{:S(2)}) collective-permute-start(f32[1,2,64,128]{3,2,0,1:T(8,128)S(1)} %slice_add_fusion.5), channel_id=1, source_target_pairs={{0,256},{4,260},{8,264},{12,268},{16,272},{20,276},{24,280},{28,28... | collective-permute-start | bytes 196616 | tf_op jit(solution)/shard_map/ppermute | solution.py:13
  (72 shorter events, 33.6 us)
Async XLA Ops:
  6.5 76.2 %all-gather.3.cloned.1.call-start = ((), (), s32[]{:S(2)}) async-start(), calls=%async_computation | async-start | bytes 2293760 | tf_op jit(solution)/shard_map/all_gather | solution.py:9
  10.2 3.8 %copy-start.1 = (f32[64,512]{1,0:T(8,128)S(1)}, f32[64,512]{1,0:T(8,128)}, u32[]{:S(2)}) copy-start(f32[64,512]{1,0:T(8,128)} %param.19) | copy-start | bytes 393220
  84.4 14.5 %collective-permute-start = (f32[7,2,64,128]{3,2,0,1:T(8,128)S(1)}, f32[7,2,64,128]{3,2,0,1:T(8,128)S(1)}, u32[]{:S(2)}, u32[]{:S(2)}) collective-permute-start(f32[7,2,64,128]{3,2,0,1:T(8,128)S(1)} %reduce_sum.9), channel_id=1, source_target_pairs={{0,4},{4,0},{8,12},{12,8},{16,20},{20,16},{24,28},{28,24},{32,36},... | collective-permute-start | bytes 1376264 | tf_op jit(solution)/shard_map/ppermute | solution.py:13
  87.1 1.2 copy-start
  99.0 13.8 %collective-permute-start.1 = (f32[6,2,64,128]{3,2,0,1:T(8,128)S(1)}, f32[6,2,64,128]{3,2,0,1:T(8,128)S(1)}, u32[]{:S(2)}, u32[]{:S(2)}) collective-permute-start(f32[6,2,64,128]{3,2,0,1:T(8,128)S(1)} %slice_add_fusion), channel_id=1, source_target_pairs={{0,8},{4,12},{8,0},{12,4},{16,24},{20,28},{24,16},{28,20},{32,40},... | collective-permute-start | bytes 1179656 | tf_op jit(solution)/shard_map/ppermute | solution.py:13
  112.9 13.9 %collective-permute-start.2 = (f32[5,2,64,128]{3,2,0,1:T(8,128)S(1)}, f32[5,2,64,128]{3,2,0,1:T(8,128)S(1)}, u32[]{:S(2)}, u32[]{:S(2)}) collective-permute-start(f32[5,2,64,128]{3,2,0,1:T(8,128)S(1)} %slice_add_fusion.1), channel_id=1, source_target_pairs={{0,16},{4,20},{8,24},{12,28},{16,0},{20,4},{24,8},{28,12},{32,48},... | collective-permute-start | bytes 983048 | tf_op jit(solution)/shard_map/ppermute | solution.py:13
  126.8 19.5 %collective-permute-start.3 = (f32[4,2,64,128]{3,2,0,1:T(8,128)S(1)}, f32[4,2,64,128]{3,2,0,1:T(8,128)S(1)}, u32[]{:S(2)}, u32[]{:S(2)}) collective-permute-start(f32[4,2,64,128]{3,2,0,1:T(8,128)S(1)} %slice_add_fusion.2), channel_id=1, source_target_pairs={{0,32},{4,36},{8,40},{12,44},{16,48},{20,52},{24,56},{28,60},{32,0... | collective-permute-start | bytes 786440 | tf_op jit(solution)/shard_map/ppermute | solution.py:13
  146.3 23.6 %collective-permute-start.4 = (f32[3,2,64,128]{3,2,0,1:T(8,128)S(1)}, f32[3,2,64,128]{3,2,0,1:T(8,128)S(1)}, u32[]{:S(2)}, u32[]{:S(2)}) collective-permute-start(f32[3,2,64,128]{3,2,0,1:T(8,128)S(1)} %slice_add_fusion.3), channel_id=1, source_target_pairs={{0,64},{4,68},{8,72},{12,76},{16,80},{20,84},{24,88},{28,92},{32,9... | collective-permute-start | bytes 589832 | tf_op jit(solution)/shard_map/ppermute | solution.py:13
  169.9 7.3 %collective-permute-start.5 = (f32[2,2,64,128]{3,2,0,1:T(8,128)S(1)}, f32[2,2,64,128]{3,2,0,1:T(8,128)S(1)}, u32[]{:S(2)}, u32[]{:S(2)}) collective-permute-start(f32[2,2,64,128]{3,2,0,1:T(8,128)S(1)} %slice_add_fusion.4), channel_id=1, source_target_pairs={{0,128},{4,132},{8,136},{12,140},{16,144},{20,148},{24,152},{28,15... | collective-permute-start | bytes 393224 | tf_op jit(solution)/shard_map/ppermute | solution.py:13
  177.3 8.3 %collective-permute-start.6 = (f32[1,2,64,128]{3,2,0,1:T(8,128)S(1)}, f32[1,2,64,128]{3,2,0,1:T(8,128)S(1)}, u32[]{:S(2)}, u32[]{:S(2)}) collective-permute-start(f32[1,2,64,128]{3,2,0,1:T(8,128)S(1)} %slice_add_fusion.5), channel_id=1, source_target_pairs={{0,256},{4,260},{8,264},{12,268},{16,272},{20,276},{24,280},{28,28... | collective-permute-start | bytes 196616 | tf_op jit(solution)/shard_map/ppermute | solution.py:13
Sparse Core Ops, SparseCore 0:
  17.3 65.3 all-gather.2
